TPU v7x, 32 devices: a whole 2x2x4 slice. The times are simulated.
32 devices in a mesh: gx: 8 (over z, y), gy: 4 (over x, core).
Axes of the slice: x: 2, y: 2, z: 4, core: 2. Of those that a mesh axis runs over, the one named last changes fastest.
Arguments:
- snapshots: bfloat16 [8, 8, 4, 2048, 512], P('gx', 'gy'), may hold values from -120 to 120
- basis: bfloat16 [8, 8, 4, 24, 2048], P('gx', 'gy'), may hold values from -0.0625 to 0.0625
- node_counts: int32 [8, 8], P('gx', 'gy'), may hold values from 1024 to 2048, as said below
- adjacency: int32 [8, 8, 3], P('gx', 'gy'), may hold values from 0 to 63, as said below
Outputs:
- operator: float32 [8, 8, 397, 24], P('gx', 'gy')
- reduced_states: float32 [8, 8, 24, 512], P('gx', 'gy')
Inputs may be any that keep to these rules, and one draw needn't show every extreme that they name: Node slot n of subdomain g is live iff n < node_counts[g]; at least 1024 slots are live, and one subdomain has all 2048 live. Subdomain (row, col) has id row * 8 + col. Each row of adjacency holds 3 distinct ids other than its own subdomain's, each within one subdomain row and one subdomain column of it.
All inputs are finite; a program needn't handle non-finite values.
Results may differ from a plain program's by a relative error of at most 0.0003.
Values sent between devices are 32-bit elements; how exact they have to be, the bound alone decides.
A program may use at most 64 MiB of HBM per device.

v0:
```python
import jax
import jax.numpy as jnp
from jax import lax
from jax.sharding import PartitionSpec as P

beta_linear = 0.5
beta_quad = 0.5


def padded_2(cells, sides, width):
    for axis, dim in sides:
        count = lax.axis_size(axis)
        ends = count - 1
        head = lax.slice_in_dim(cells, 0, width, axis=dim)
        tail = lax.slice_in_dim(cells, cells.shape[dim] - width, cells.shape[dim], axis=dim)
        cells = jnp.concatenate(
            [
                lax.ppermute(tail, axis, [(i, (i + 1) % count) for i in range(ends)]),
                cells,
                lax.ppermute(head, axis, [((i + 1) % count, i) for i in range(ends)]),
            ],
            axis=dim,
        )
    return cells


def build_features(state, near):
    ranks = state.shape[1]
    steps = state.shape[2]
    pieces = [
        jnp.ones((state.shape[0], 1, steps), jnp.float32),
        state,
        near.reshape(state.shape[0], -1, steps),
    ]
    for first in range(ranks):
        pieces.append(state[:, first : first + 1] * state[:, first:])
    return jnp.concatenate(pieces, axis=1)


def pick_rows(pieces, links):
    ids = jnp.arange(pieces.shape[0], dtype=jnp.int32)
    hits = (links[:, :, None] == ids[None, None, :]).astype(jnp.float32)
    return jnp.einsum("sbn,nrk->sbrk", hits, pieces, precision=lax.Precision.HIGHEST)


def solve_one(gram, rhs):
    factor = jnp.linalg.cholesky(gram)
    middle = jax.scipy.linalg.solve_triangular(factor, rhs, lower=True)
    return jax.scipy.linalg.solve_triangular(factor, middle, lower=True, trans=1)


def body(snapshots, basis, node_counts, adjacency):
    values = snapshots[0]
    modes = basis[0]
    counts = node_counts[0]
    links = adjacency[0]
    columns = values.shape[0]
    slots = values.shape[2]
    steps = values.shape[3]
    ranks = modes.shape[2]
    live = jnp.arange(slots, dtype=jnp.int32)[None, :] < counts[:, None]
    masked = modes * live.astype(jnp.bfloat16)[:, None, None, :]
    proj = jnp.einsum("svrp,svpk->svrk", masked, values, preferred_element_type=jnp.float32)
    slotsq = jnp.einsum("svpk,svpk->svp", values, values, preferred_element_type=jnp.float32)
    squares = jnp.sum(slotsq * live.astype(jnp.float32)[:, None, :], axis=(0, 2))
    nodes = jnp.sum(counts.astype(jnp.float32))
    total_subs = lax.axis_size("gx") * lax.axis_size("gy") * columns
    grid_cols = columns * lax.axis_size("gy")
    near_row = links // grid_cols
    near_col = links % grid_cols
    local = (near_row - lax.axis_index("gx") + 1) * (columns + 2) + (
        near_col - lax.axis_index("gy") * columns + 1
    )
    cross = jnp.einsum("svrk,swrk->vw", proj, proj, precision=lax.Precision.HIGHEST)
    sq_all, nodes_all, cross_all = lax.psum((squares, nodes, cross), ("gx", "gy"))
    scale = jnp.sqrt(sq_all / (nodes_all * steps) + 1e-06)
    states = jnp.sum(proj / scale[None, :, None, None], axis=1)
    gnorm = jnp.sum(cross_all / (scale[:, None] * scale[None, :])) / (total_subs * ranks * steps)
    padded = padded_2(states[None], (("gx", 0), ("gy", 1)), 1)
    flat = padded.reshape(-1, ranks, steps)
    near = pick_rows(flat, local)
    nbrs = links.shape[1]
    feats = build_features(states, near)
    past = feats[:, :, :-1]
    nlin = 1 + ranks + nbrs * ranks
    nquad = ranks * (ranks + 1) // 2
    reg_diag = steps * jnp.concatenate(
        [
            jnp.full((nlin,), beta_linear, jnp.float32) * gnorm,
            jnp.full((nquad,), beta_quad, jnp.float32) * gnorm * gnorm,
        ]
    )
    gram = (
        jnp.einsum("sfk,sgk->sfg", past, past, precision=lax.Precision.HIGHEST)
        + jnp.diag(reg_diag)[None]
    )
    rhs = jnp.einsum("sfk,srk->sfr", past, states[:, :, 1:], precision=lax.Precision.HIGHEST)
    operator = jax.vmap(solve_one)(gram, rhs)
    return (operator[None], states[None])


def solution(mesh):
    in_specs = (
        P("gx", "gy", None, None, None),
        P("gx", "gy", None, None, None),
        P("gx", "gy"),
        P("gx", "gy", None),
    )
    out_specs = (P("gx", "gy", None, None), P("gx", "gy", None, None))
    return jax.shard_map(body, mesh=mesh, in_specs=in_specs, out_specs=out_specs, check_vma=False)
```

profile of v0, /device:TPU:1, one launch (start us, length us, event | category | flops | bytes accessed | tf_op | source)
XLA Modules:
  0.0 338.5 jit_solution(2032630812765545449)
XLA Ops:
  1.4 7.5 %fusion = f32[2,4,2048]{2,1,0:T(4,128)S(1)} fusion(bf16[1,2,4,2048,512]{4,3,2,1,0:T(8,128)(2,1)} %param.4), kind=kLoop, calls=%fused_computation.3 | loop fusion | flops 25149440 | bytes 16842752 | tf_op jit(solution)/shard_map/svpk,svpk->svp/dot_general | solution.py:64
  8.9 3.2 copy-done
  12.0 3.4 %fusion.1 = f32[2,4,24,512]{3,2,1,0:T(8,128)S(1)} fusion(bf16[1,2,4,2048,512]{4,3,2,1,0:T(8,128)(2,1)S(1)} %copy-done, bf16[1,2,4,24,2048]{4,3,2,1,0:T(8,128)(2,1)} %param.5, bf16[2,2048]{1,0:T(2,128)(2,1)S(1)} %get-tuple-element.61), kind=kOutput, calls=%fused_computation.4 | convolution fusion | flops 403046400 | bytes 17965056 | tf_op jit(solution)/shard_map/svrp,svpk->svrk/dot_general | solution.py:63
  15.5 1.9 convolution_bitcast_fusion
  18.1 40.9 %all-reduce.4 = (f32[4]{0:T(128)S(1)}, f32[]{:T(128)}, f32[4,4]{1,0:T(4,128)S(1)}) all-reduce(f32[4]{0:T(128)S(1)} %multiply_reduce_fusion, f32[]{:T(128)} %convert_reduce_fusion, f32[4,4]{1,0:T(4,128)S(1)} %convolution_bitcast_fusion), channel_id=1, replica_groups=mesh['gx'=8,'gy'=4] {'gx','gy'}, use_global_device_ids=true, to_apply=%region_1.0 | all-reduce | flops 21 | bytes 168 | tf_op jit(solution)/shard_map/psum | solution.py:75
  59.8 1.3 collective-permute-start.1
  61.1 4.0 %collective-permute-start = (f32[1,2,24,512]{3,2,1,0:T(8,128)S(1)}, f32[1,2,24,512]{3,2,1,0:T(8,128)S(1)}, u32[]{:S(2)}, u32[]{:S(2)}) collective-permute-start(f32[1,2,24,512]{3,2,1,0:T(8,128)S(1)} %bitcast.156), channel_id=1, source_target_pairs={{0,4},{4,8},{8,12},{12,16},{16,20},{20,24},{24,28},{1,5},{5,9},{9,... | collective-permute-start | bytes 294920 | tf_op jit(solution)/shard_map/ppermute | solution.py:18
  74.7 1.4 fusion.9
  76.7 5.7 %collective-permute-start.2 = (f32[3,1,24,512]{3,2,1,0:T(8,128)S(1)}, f32[3,1,24,512]{3,2,1,0:T(8,128)S(1)}, u32[]{:S(2)}, u32[]{:S(2)}) collective-permute-start(f32[3,1,24,512]{3,2,1,0:T(8,128)S(1)} %get-tuple-element.26), channel_id=1, source_target_pairs={{0,1},{1,2},{2,3},{4,5},{5,6},{6,7},{8,9},{9,10},{10,11},{12,13},{... | collective-permute-start | bytes 442376 | tf_op jit(solution)/shard_map/ppermute | solution.py:18
  82.4 2.4 collective-permute-start.3
  86.1 2.7 collective-permute-done.3
  89.8 8.0 %concatenate.48 = f32[2,397,512]{2,1,0:T(8,128)S(1)} concatenate(f32[2,1,512]{2,1,0:T(1,128)S(1)} %broadcast_in_dim.45, f32[2,24,512]{2,1,0:T(8,128)S(1)} %divide_reduce_fusion, f32[2,72,512]{2,1,0:T(8,128)S(1)} %bitcast.161, f32[2,24,512]{2,1,0:T(8,128)S(1)} %broadcast_multiply_fusion, f32[2,23,512]{2,1,0:T(8,128)S(1)} %slice_multiply_fusion.6, ...), dimensions={1} | concatenate | bytes 3252224 | tf_op jit(solution)/shard_map/concatenate | solution.py:37
  97.8 1.5 fusion.5
  99.3 2.8 fusion.7
  102.9 2.0 fusion.4
  104.9 1.2 copy-done.2
  106.1 23.5 %custom-call.38 = f32[2,128,128]{2,1,0:T(8,128)S(1)} custom-call(f32[2,128,128]{2,1,0:T(8,128)S(1)} %cholesky.281), custom_call_target="Cholesky" | custom-call | tf_op jit(solution)/shard_map/vmap(jit(cholesky))/cholesky | solution.py:47
  129.6 19.8 %custom-call.39 = f32[2,1,128,128]{2,3,1,0:T(8,128)S(1)} custom-call(f32[2,1,128,128]{3,2,1,0:T(8,128)S(1)} %select_bitcast_fusion.2), custom_call_target="InvertDiagBlocksLowerTriangular" | custom-call | tf_op jit(solution)/shard_map/vmap(jit(cholesky))/cholesky | solution.py:47
  149.6 1.4 constant_dynamic-update-slice_fusion.3
  151.0 1.4 convolution_subtract_fusion
  152.4 23.5 %custom-call.40 = f32[2,128,128]{2,1,0:T(8,128)S(1)} custom-call(f32[2,128,128]{2,1,0:T(8,128)S(1)} %cholesky.285), custom_call_target="Cholesky" | custom-call | tf_op jit(solution)/shard_map/vmap(jit(cholesky))/cholesky | solution.py:47
  175.9 19.7 %custom-call.41 = f32[2,1,128,128]{2,3,1,0:T(8,128)S(1)} custom-call(f32[2,1,128,128]{3,2,1,0:T(8,128)S(1)} %get-tuple-element.30), custom_call_target="InvertDiagBlocksLowerTriangular" | custom-call | tf_op jit(solution)/shard_map/vmap(jit(cholesky))/cholesky | solution.py:47
  195.9 1.3 convolution_subtract_fusion.1
  197.2 23.7 %custom-call.42 = f32[2,128,128]{2,1,0:T(8,128)S(1)} custom-call(f32[2,128,128]{2,1,0:T(8,128)S(1)} %cholesky.290), custom_call_target="Cholesky" | custom-call | tf_op jit(solution)/shard_map/vmap(jit(cholesky))/cholesky | solution.py:47
  221.3 19.7 %custom-call.43 = f32[2,1,128,128]{2,3,1,0:T(8,128)S(1)} custom-call(f32[2,1,128,128]{3,2,1,0:T(8,128)S(1)} %get-tuple-element.28), custom_call_target="InvertDiagBlocksLowerTriangular" | custom-call | tf_op jit(solution)/shard_map/vmap(jit(cholesky))/cholesky | solution.py:47
  242.1 2.4 custom-call.44
  244.7 1.3 select_select_fusion
  246.0 7.9 %while.1 = (s32[]{:T(128)}, f32[2,397,397]{2,1,0:T(8,128)S(1)}, s32[3,2]{0,1:T(2,128)S(1)}, f32[3,2,128,128]{3,2,0,1:T(8,128)}, s32[]{:T(128)}) while((s32[]{:T(128)}, f32[2,397,397]{2,1,0:T(8,128)S(1)}, s32[3,2]{0,1:T(2,128)S(1)}, f32[3,2,128,128]{3,2,0,1:T(8,128)}, s32[]{:T(128)}) %tuple.67), condition=%wide.while_cond, body=%wide.while_body.sunk | while | flops 2 | bytes 263277 | solution.py:49
  246.7 2.0 bitcast_dynamic-update-slice_fusion.2
  249.3 2.0 bitcast_dynamic-update-slice_fusion.2
  252.0 2.0 bitcast_dynamic-update-slice_fusion.2
  255.1 78.6 %custom-call.45 = f32[2,4,128,128]{2,3,1,0:T(8,128)S(1)} custom-call(f32[2,4,128,128]{3,2,1,0:T(8,128)S(1)} %pad_maximum_fusion.1), custom_call_target="InvertDiagBlocksLowerTriangular" | custom-call | tf_op jit(solution)/shard_map/vmap(jit(_solve_triangular))/triangular_solve | solution.py:49
  (122 shorter events, 22.4 us)
Async XLA Ops:
  1.4 10.7 %copy-start = (bf16[1,2,4,2048,512]{4,3,2,1,0:T(8,128)(2,1)S(1)}, bf16[1,2,4,2048,512]{4,3,2,1,0:T(8,128)(2,1)}, u32[]{:S(2)}) copy-start(bf16[1,2,4,2048,512]{4,3,2,1,0:T(8,128)(2,1)} %param.4) | copy-start | bytes 50331652
  12.0 5.5 %copy-start.7 = (s32[1,2]{1,0:T(1,128)S(1)}, s32[1,2]{1,0:T(1,128)}, u32[]{:S(2)}) copy-start(s32[1,2]{1,0:T(1,128)} %param.6) | copy-start | bytes 28
  59.8 38.0 %copy-start.1 = (f32[2,24,512]{2,1,0:T(8,128)}, f32[2,24,512]{2,1,0:T(8,128)S(1)}, u32[]{:S(2)}) copy-start(f32[2,24,512]{2,1,0:T(8,128)S(1)} %divide_reduce_fusion) | copy-start | bytes 294916
  59.8 16.9 %collective-permute-start.1 = (f32[1,2,24,512]{3,2,1,0:T(8,128)S(1)}, f32[1,2,24,512]{3,2,1,0:T(8,128)S(1)}, u32[]{:S(2)}, u32[]{:S(2)}) collective-permute-start(f32[1,2,24,512]{3,2,1,0:T(8,128)S(1)} %bitcast.155), channel_id=1, source_target_pairs={{4,0},{8,4},{12,8},{16,12},{20,16},{24,20},{28,24},{5,1},{9,5},{13... | collective-permute-start | bytes 294920 | tf_op jit(solution)/shard_map/ppermute | solution.py:20
  61.1 15.6 %collective-permute-start = (f32[1,2,24,512]{3,2,1,0:T(8,128)S(1)}, f32[1,2,24,512]{3,2,1,0:T(8,128)S(1)}, u32[]{:S(2)}, u32[]{:S(2)}) collective-permute-start(f32[1,2,24,512]{3,2,1,0:T(8,128)S(1)} %bitcast.156), channel_id=1, source_target_pairs={{0,4},{4,8},{8,12},{12,16},{16,20},{20,24},{24,28},{1,5},{5,9},{9,... | collective-permute-start | bytes 294920 | tf_op jit(solution)/shard_map/ppermute | solution.py:18
  74.4 1.7 copy-start.6
  76.7 9.4 %collective-permute-start.2 = (f32[3,1,24,512]{3,2,1,0:T(8,128)S(1)}, f32[3,1,24,512]{3,2,1,0:T(8,128)S(1)}, u32[]{:S(2)}, u32[]{:S(2)}) collective-permute-start(f32[3,1,24,512]{3,2,1,0:T(8,128)S(1)} %get-tuple-element.26), channel_id=1, source_target_pairs={{0,1},{1,2},{2,3},{4,5},{5,6},{6,7},{8,9},{9,10},{10,11},{12,13},{... | collective-permute-start | bytes 442376 | tf_op jit(solution)/shard_map/ppermute | solution.py:18
  82.4 6.5 %collective-permute-start.3 = (f32[3,1,24,512]{3,2,1,0:T(8,128)S(1)}, f32[3,1,24,512]{3,2,1,0:T(8,128)S(1)}, u32[]{:S(2)}, u32[]{:S(2)}) collective-permute-start(f32[3,1,24,512]{3,2,1,0:T(8,128)S(1)} %get-tuple-element.27), channel_id=1, source_target_pairs={{1,0},{2,1},{3,2},{5,4},{6,5},{7,6},{9,8},{10,9},{11,10},{13,12},{... | collective-permute-start | bytes 442376 | tf_op jit(solution)/shard_map/ppermute | solution.py:20
  104.9 1.2 copy-start.2
  151.0 69.9 %copy-start.4 = (pred[128,128]{1,0:T(8,128)(4,1)S(1)}, pred[128,128]{1,0:T(8,128)(4,1)}, u32[]{:S(2)}) copy-start(pred[128,128]{1,0:T(8,128)(4,1)} %get-tuple-element.87) | copy-start | bytes 49156
  152.4 92.1 %copy-start.5 = (pred[13,13]{1,0:T(8,128)(4,1)S(1)}, pred[13,13]{1,0:T(8,128)(4,1)}, u32[]{:S(2)}) copy-start(pred[13,13]{1,0:T(8,128)(4,1)} %iota_compare_fusion.8) | copy-start | bytes 511
  244.7 1.3 copy-start.8
  244.7 9.2 %copy-start.3 = (f32[128,115]{1,0:T(8,128)S(1)}, f32[128,115]{1,0:T(8,128)}, u32[]{:S(2)}) copy-start(f32[128,115]{1,0:T(8,128)} %pad_convert_fusion) | copy-start | bytes 176644
where the time goes:
time: 344 us; the launch traced here: 339 us
  other arithmetic  236 us (69%)
  blocking collectives  40.9 us (12%)
  local copies, waits for them, and re-layouts  21.6 us (6%)
  matrix products  19.7 us (6%)
  starting transfers between devices  13.3 us (4%)
  between operations  4.19 us (1%)
    another operation x18, other arithmetic, solve_one(): factor = jnp.linalg.cholesky(gram)  134 us
    another operation x8, other arithmetic, solve_one(): jax.scipy.linalg.solve_triangular(factor, middle, lower=True, trans=1)  83 us
    psum x1, blocking collectives, body(): lax.psum((squares, nodes, cross), ('gx', 'gy'))  40.9 us
    ppermute x2, starting transfers between devices, padded_2(): lax.ppermute(tail, axis, [(i, (i + 1) % count) for i in range(ends)])  9.65 us
    concatenate x1, local copies, waits for them, and re-layouts, build_features(): return jnp.concatenate(pieces, axis=1)  8.01 us
    another operation x9, local copies, waits for them, and re-layouts  7.89 us
    dot_general x1, other arithmetic, body(): jnp.einsum('svpk,svpk->svp', values, values, preferred_element_type=jnp.f...  7.47 us
  transfers between devices with their start and end apart: 4, of which 1 were waited for; matrix products, arithmetic and copies ran while one was open for 3% of the time, Pallas kernels for 0%

commit v1 on v0

--- a/solution.py
+++ b/solution.py
@@ -72,7 +72,7 @@
         near_col - lax.axis_index("gy") * columns + 1
     )
     cross = jnp.einsum("svrk,swrk->vw", proj, proj, precision=lax.Precision.HIGHEST)
-    sq_all, nodes_all, cross_all = lax.psum((squares, nodes, cross), ("gx", "gy"))
+    sq_all, nodes_all, cross_all = lax.psum(lax.psum((squares, nodes, cross), "gy"), "gx")
     scale = jnp.sqrt(sq_all / (nodes_all * steps) + 1e-06)
     states = jnp.sum(proj / scale[None, :, None, None], axis=1)
     gnorm = jnp.sum(cross_all / (scale[:, None] * scale[None, :])) / (total_subs * ranks * steps)

time: 344 us -> 331 us (0.962)
  blocking collectives: 40.9 us -> 25.6 us
    psum x1 -> x2, blocking collectives: 40.9 us -> 25.6 us  [the longest x1 18.7 us: body(): lax.psum(lax.psum((squares, nodes, cross), 'gy'), 'gx')]
where the time goes in v1:
time: 331 us; the launch traced here: 326 us
  other arithmetic  236 us (71%)
  blocking collectives  25.6 us (8%)
  local copies, waits for them, and re-layouts  21.6 us (7%)
  matrix products  19.7 us (6%)
  starting transfers between devices  15.9 us (5%)
  between operations  4.19 us (1%)
    another operation x18, other arithmetic, solve_one(): factor = jnp.linalg.cholesky(gram)  134 us
    another operation x8, other arithmetic, solve_one(): jax.scipy.linalg.solve_triangular(factor, middle, lower=True, trans=1)  83 us
    psum x1, blocking collectives, body(): lax.psum(lax.psum((squares, nodes, cross), 'gy'), 'gx')  18.7 us
    ppermute x2, starting transfers between devices, padded_2(): lax.ppermute(tail, axis, [(i, (i + 1) % count) for i in range(ends)])  12.2 us
    concatenate x1, local copies, waits for them, and re-layouts, build_features(): return jnp.concatenate(pieces, axis=1)  8.01 us
    another operation x9, local copies, waits for them, and re-layouts  7.89 us
    dot_general x1, other arithmetic, body(): jnp.einsum('svpk,svpk->svp', values, values, preferred_element_type=jnp.f...  7.47 us
    psum x1, blocking collectives, body(): lax.psum((squares, nodes, cross), 'gy')  6.98 us
  transfers between devices with their start and end apart: 4, of which 1 were waited for; matrix products, arithmetic and copies ran while one was open for 3% of the time, Pallas kernels for 0%

profile of v1, /device:TPU:1, one launch (start us, length us, event | category | flops | bytes accessed | tf_op | source)
XLA Modules:
  0.0 325.9 jit_solution(4656764787365097028)
XLA Ops:
  1.4 7.5 %fusion = f32[2,4,2048]{2,1,0:T(4,128)S(1)} fusion(bf16[1,2,4,2048,512]{4,3,2,1,0:T(8,128)(2,1)} %param.4), kind=kLoop, calls=%fused_computation.3 | loop fusion | flops 25149440 | bytes 16842752 | tf_op jit(solution)/shard_map/svpk,svpk->svp/dot_general | solution.py:64
  8.9 3.2 copy-done
  12.0 3.4 %fusion.1 = f32[2,4,24,512]{3,2,1,0:T(8,128)S(1)} fusion(bf16[1,2,4,2048,512]{4,3,2,1,0:T(8,128)(2,1)S(1)} %copy-done, bf16[1,2,4,24,2048]{4,3,2,1,0:T(8,128)(2,1)} %param.5, bf16[2,2048]{1,0:T(2,128)(2,1)S(1)} %get-tuple-element.64), kind=kOutput, calls=%fused_computation.4 | convolution fusion | flops 403046400 | bytes 17965056 | tf_op jit(solution)/shard_map/svrp,svpk->svrk/dot_general | solution.py:63
  15.5 1.9 convolution_bitcast_fusion
  18.1 7.0 %all-reduce.5 = (f32[4]{0:T(128)S(1)}, f32[]{:T(128)}, f32[4,4]{1,0:T(4,128)S(1)}) all-reduce(f32[4]{0:T(128)S(1)} %multiply_reduce_fusion, f32[]{:T(128)} %convert_reduce_fusion, f32[4,4]{1,0:T(4,128)S(1)} %convolution_bitcast_fusion), channel_id=1, replica_groups=mesh['gx'=8,'gy'=4] {'gy'}, use_global_device_ids=true, to_apply=%region_1.0 | all-reduce | flops 21 | bytes 168 | tf_op jit(solution)/shard_map/psum | solution.py:75
  25.1 18.7 %all-reduce.4 = (f32[4]{0:T(128)S(1)}, f32[]{:T(128)}, f32[4,4]{1,0:T(4,128)S(1)}) all-reduce(f32[4]{0:T(128)S(1)} %get-tuple-element.24, f32[]{:T(128)} %get-tuple-element.25, f32[4,4]{1,0:T(4,128)S(1)} %get-tuple-element.26), channel_id=1, replica_groups=mesh['gx'=8,'gy'=4] {'gx'}, use_global_device_ids=true, to_apply=%region_2.3 | all-reduce | flops 21 | bytes 168 | tf_op jit(solution)/shard_map/psum | solution.py:75
  44.6 1.3 collective-permute-start.1
  45.9 4.0 %collective-permute-start = (f32[1,2,24,512]{3,2,1,0:T(8,128)S(1)}, f32[1,2,24,512]{3,2,1,0:T(8,128)S(1)}, u32[]{:S(2)}, u32[]{:S(2)}) collective-permute-start(f32[1,2,24,512]{3,2,1,0:T(8,128)S(1)} %bitcast.156), channel_id=1, source_target_pairs={{0,4},{4,8},{8,12},{12,16},{16,20},{20,24},{24,28},{1,5},{5,9},{9,... | collective-permute-start | bytes 294920 | tf_op jit(solution)/shard_map/ppermute | solution.py:18
  59.5 1.4 fusion.9
  61.5 8.2 %collective-permute-start.2 = (f32[3,1,24,512]{3,2,1,0:T(8,128)S(1)}, f32[3,1,24,512]{3,2,1,0:T(8,128)S(1)}, u32[]{:S(2)}, u32[]{:S(2)}) collective-permute-start(f32[3,1,24,512]{3,2,1,0:T(8,128)S(1)} %get-tuple-element.29), channel_id=1, source_target_pairs={{0,1},{1,2},{2,3},{4,5},{5,6},{6,7},{8,9},{9,10},{10,11},{12,13},{... | collective-permute-start | bytes 442376 | tf_op jit(solution)/shard_map/ppermute | solution.py:18
  69.7 2.4 collective-permute-start.3
  73.4 2.7 collective-permute-done.3
  77.1 8.0 %concatenate.48 = f32[2,397,512]{2,1,0:T(8,128)S(1)} concatenate(f32[2,1,512]{2,1,0:T(1,128)S(1)} %broadcast_in_dim.45, f32[2,24,512]{2,1,0:T(8,128)S(1)} %divide_reduce_fusion, f32[2,72,512]{2,1,0:T(8,128)S(1)} %bitcast.161, f32[2,24,512]{2,1,0:T(8,128)S(1)} %broadcast_multiply_fusion, f32[2,23,512]{2,1,0:T(8,128)S(1)} %slice_multiply_fusion.6, ...), dimensions={1} | concatenate | bytes 3252224 | tf_op jit(solution)/shard_map/concatenate | solution.py:37
  85.1 1.5 fusion.5
  86.7 2.8 fusion.7
  90.2 2.0 fusion.4
  93.4 23.5 %custom-call.38 = f32[2,128,128]{2,1,0:T(8,128)S(1)} custom-call(f32[2,128,128]{2,1,0:T(8,128)S(1)} %cholesky.281), custom_call_target="Cholesky" | custom-call | tf_op jit(solution)/shard_map/vmap(jit(cholesky))/cholesky | solution.py:47
  116.9 19.8 %custom-call.39 = f32[2,1,128,128]{2,3,1,0:T(8,128)S(1)} custom-call(f32[2,1,128,128]{3,2,1,0:T(8,128)S(1)} %select_bitcast_fusion.2), custom_call_target="InvertDiagBlocksLowerTriangular" | custom-call | tf_op jit(solution)/shard_map/vmap(jit(cholesky))/cholesky | solution.py:47
  137.0 1.4 constant_dynamic-update-slice_fusion.3
  138.3 1.4 convolution_subtract_fusion
  139.7 23.5 %custom-call.40 = f32[2,128,128]{2,1,0:T(8,128)S(1)} custom-call(f32[2,128,128]{2,1,0:T(8,128)S(1)} %cholesky.285), custom_call_target="Cholesky" | custom-call | tf_op jit(solution)/shard_map/vmap(jit(cholesky))/cholesky | solution.py:47
  163.2 19.7 %custom-call.41 = f32[2,1,128,128]{2,3,1,0:T(8,128)S(1)} custom-call(f32[2,1,128,128]{3,2,1,0:T(8,128)S(1)} %get-tuple-element.33), custom_call_target="InvertDiagBlocksLowerTriangular" | custom-call | tf_op jit(solution)/shard_map/vmap(jit(cholesky))/cholesky | solution.py:47
  183.2 1.3 convolution_subtract_fusion.1
  184.6 23.7 %custom-call.42 = f32[2,128,128]{2,1,0:T(8,128)S(1)} custom-call(f32[2,128,128]{2,1,0:T(8,128)S(1)} %cholesky.290), custom_call_target="Cholesky" | custom-call | tf_op jit(solution)/shard_map/vmap(jit(cholesky))/cholesky | solution.py:47
  208.6 19.7 %custom-call.43 = f32[2,1,128,128]{2,3,1,0:T(8,128)S(1)} custom-call(f32[2,1,128,128]{3,2,1,0:T(8,128)S(1)} %get-tuple-element.31), custom_call_target="InvertDiagBlocksLowerTriangular" | custom-call | tf_op jit(solution)/shard_map/vmap(jit(cholesky))/cholesky | solution.py:47
  229.5 2.4 custom-call.44
  232.0 1.3 select_select_fusion
  233.4 7.9 %while.1 = (s32[]{:T(128)}, f32[2,397,397]{2,1,0:T(8,128)S(1)}, s32[3,2]{0,1:T(2,128)S(1)}, f32[3,2,128,128]{3,2,0,1:T(8,128)}, s32[]{:T(128)}) while((s32[]{:T(128)}, f32[2,397,397]{2,1,0:T(8,128)S(1)}, s32[3,2]{0,1:T(2,128)S(1)}, f32[3,2,128,128]{3,2,0,1:T(8,128)}, s32[]{:T(128)}) %tuple.67), condition=%wide.while_cond, body=%wide.while_body.sunk | while | flops 2 | bytes 263277 | solution.py:49
  234.0 2.0 bitcast_dynamic-update-slice_fusion.2
  236.7 2.0 bitcast_dynamic-update-slice_fusion.2
  239.3 2.0 bitcast_dynamic-update-slice_fusion.2
  242.4 78.6 %custom-call.45 = f32[2,4,128,128]{2,3,1,0:T(8,128)S(1)} custom-call(f32[2,4,128,128]{3,2,1,0:T(8,128)S(1)} %pad_maximum_fusion.1), custom_call_target="InvertDiagBlocksLowerTriangular" | custom-call | tf_op jit(solution)/shard_map/vmap(jit(_solve_triangular))/triangular_solve | solution.py:49
  (123 shorter events, 23.6 us)
Async XLA Ops:
  1.4 10.7 %copy-start = (bf16[1,2,4,2048,512]{4,3,2,1,0:T(8,128)(2,1)S(1)}, bf16[1,2,4,2048,512]{4,3,2,1,0:T(8,128)(2,1)}, u32[]{:S(2)}) copy-start(bf16[1,2,4,2048,512]{4,3,2,1,0:T(8,128)(2,1)} %param.4) | copy-start | bytes 50331652
  12.0 5.5 %copy-start.7 = (s32[1,2]{1,0:T(1,128)S(1)}, s32[1,2]{1,0:T(1,128)}, u32[]{:S(2)}) copy-start(s32[1,2]{1,0:T(1,128)} %param.6) | copy-start | bytes 28
  44.6 40.6 %copy-start.1 = (f32[2,24,512]{2,1,0:T(8,128)}, f32[2,24,512]{2,1,0:T(8,128)S(1)}, u32[]{:S(2)}) copy-start(f32[2,24,512]{2,1,0:T(8,128)S(1)} %divide_reduce_fusion) | copy-start | bytes 294916
  44.6 16.9 %collective-permute-start.1 = (f32[1,2,24,512]{3,2,1,0:T(8,128)S(1)}, f32[1,2,24,512]{3,2,1,0:T(8,128)S(1)}, u32[]{:S(2)}, u32[]{:S(2)}) collective-permute-start(f32[1,2,24,512]{3,2,1,0:T(8,128)S(1)} %bitcast.155), channel_id=1, source_target_pairs={{4,0},{8,4},{12,8},{16,12},{20,16},{24,20},{28,24},{5,1},{9,5},{13... | collective-permute-start | bytes 294920 | tf_op jit(solution)/shard_map/ppermute | solution.py:20
  45.9 15.6 %collective-permute-start = (f32[1,2,24,512]{3,2,1,0:T(8,128)S(1)}, f32[1,2,24,512]{3,2,1,0:T(8,128)S(1)}, u32[]{:S(2)}, u32[]{:S(2)}) collective-permute-start(f32[1,2,24,512]{3,2,1,0:T(8,128)S(1)} %bitcast.156), channel_id=1, source_target_pairs={{0,4},{4,8},{8,12},{12,16},{16,20},{20,24},{24,28},{1,5},{5,9},{9,... | collective-permute-start | bytes 294920 | tf_op jit(solution)/shard_map/ppermute | solution.py:18
  59.2 1.7 copy-start.6
  61.5 11.9 %collective-permute-start.2 = (f32[3,1,24,512]{3,2,1,0:T(8,128)S(1)}, f32[3,1,24,512]{3,2,1,0:T(8,128)S(1)}, u32[]{:S(2)}, u32[]{:S(2)}) collective-permute-start(f32[3,1,24,512]{3,2,1,0:T(8,128)S(1)} %get-tuple-element.29), channel_id=1, source_target_pairs={{0,1},{1,2},{2,3},{4,5},{5,6},{6,7},{8,9},{9,10},{10,11},{12,13},{... | collective-permute-start | bytes 442376 | tf_op jit(solution)/shard_map/ppermute | solution.py:18
  69.7 6.5 %collective-permute-start.3 = (f32[3,1,24,512]{3,2,1,0:T(8,128)S(1)}, f32[3,1,24,512]{3,2,1,0:T(8,128)S(1)}, u32[]{:S(2)}, u32[]{:S(2)}) collective-permute-start(f32[3,1,24,512]{3,2,1,0:T(8,128)S(1)} %get-tuple-element.30), channel_id=1, source_target_pairs={{1,0},{2,1},{3,2},{5,4},{6,5},{7,6},{9,8},{10,9},{11,10},{13,12},{... | collective-permute-start | bytes 442376 | tf_op jit(solution)/shard_map/ppermute | solution.py:20
  92.2 1.2 copy-start.2
  138.3 69.9 %copy-start.4 = (pred[128,128]{1,0:T(8,128)(4,1)S(1)}, pred[128,128]{1,0:T(8,128)(4,1)}, u32[]{:S(2)}) copy-start(pred[128,128]{1,0:T(8,128)(4,1)} %get-tuple-element.90) | copy-start | bytes 49156
  139.7 92.1 %copy-start.5 = (pred[13,13]{1,0:T(8,128)(4,1)S(1)}, pred[13,13]{1,0:T(8,128)(4,1)}, u32[]{:S(2)}) copy-start(pred[13,13]{1,0:T(8,128)(4,1)} %iota_compare_fusion.8) | copy-start | bytes 511
  232.0 1.3 copy-start.8
  232.0 9.2 %copy-start.3 = (f32[128,115]{1,0:T(8,128)S(1)}, f32[128,115]{1,0:T(8,128)}, u32[]{:S(2)}) copy-start(f32[128,115]{1,0:T(8,128)} %pad_convert_fusion) | copy-start | bytes 176644
